TPU v7x, 32 devices: a whole 2x2x4 slice. The times are simulated.
32 devices in a mesh: ba: 8 (over z, x), ka: 4 (over y, core).
Axes of the slice: x: 2, y: 2, z: 4, core: 2. Of those that a mesh axis runs over, the one named last changes fastest.
Arguments:
- emb_one: bfloat16 [8192, 128], P('ba'), may hold values from -8 to 8, as said below
- emb_two: bfloat16 [8192, 128], P('ba'), may hold values from -8 to 8, as said below
- prototypes: float32 [3000, 128], P('ka', 'ba'), may hold values from -6 to 6, as said below
Outputs:
- assignment_weights: float32 [8192, 3000], P('ba', 'ka')
- row_loss: float32 [8192], P('ba')
Inputs may be any that keep to these rules, and one draw needn't show every extreme that they name: `prototypes`: prototype entries are finite and lie within the stated range. `emb_one`: embedding entries are finite and lie within the stated range; rows are not zero. `emb_two`: embedding entries are finite and lie within the stated range; rows are not zero.
All inputs are finite; a program needn't handle non-finite values.
Results may differ from a plain program's by a relative error of at most 0.0003.
Values sent between devices are 32-bit elements.
A program may use at most 64 MiB of HBM per device.

v0:
```python
import jax
import jax.numpy as jnp
from jax import lax
from jax.sharding import PartitionSpec as P

K = 3000
REPEAT_COUNT = 3
TEMP_CODE = 0.05
TEMP_PRED = 0.1


def unit_rows(values):
    values = values.astype(jnp.float32)
    factor = lax.rsqrt(jnp.sum(values * values, axis=1, keepdims=True))
    return (values * factor).astype(jnp.bfloat16)


def vector_columns(current):
    kernel, col_scale, row_scale = current
    return (
        jnp.sum(kernel[0] * row_scale[0][:, None], axis=0),
        jnp.sum(kernel[1] * row_scale[1][:, None], axis=0),
    )


def vector_by_columns(current, totals):
    return (current[0], (1.0 / totals[0], 1.0 / totals[1]), current[2])


def vector_samples(current):
    kernel, col_scale, row_scale = current
    return (
        jnp.sum(kernel[0] * col_scale[0][None, :], axis=1),
        jnp.sum(kernel[1] * col_scale[1][None, :], axis=1),
    )


def vector_by_samples(current, totals):
    return (current[0], current[1], (1.0 / totals[0], 1.0 / totals[1]))


def vector_raw(current):
    kernel, col_scale, row_scale = current
    return (
        kernel[0] * col_scale[0][None, :] * row_scale[0][:, None],
        kernel[1] * col_scale[1][None, :] * row_scale[1][:, None],
    )


def body(emb_one, emb_two, prototypes):
    gathered = lax.all_gather(prototypes, "ba", axis=1, tiled=True)
    centers = unit_rows(gathered)
    first_view_logits = jnp.dot(unit_rows(emb_one), centers.T, preferred_element_type=jnp.float32)
    second_view_logits = jnp.dot(unit_rows(emb_two), centers.T, preferred_element_type=jnp.float32)
    kernel = (jnp.exp(first_view_logits / TEMP_CODE), jnp.exp(second_view_logits / TEMP_CODE))
    column_part, column_apply = (vector_columns, vector_by_columns)
    sample_part, sample_apply, raw_matrix = (vector_samples, vector_by_samples, vector_raw)
    col_ones = jnp.ones((first_view_logits.shape[1],), jnp.float32)
    row_ones = jnp.ones((first_view_logits.shape[0],), jnp.float32)
    current = (kernel, (col_ones, col_ones), (row_ones, row_ones))
    for iteration in range(REPEAT_COUNT):
        partial_sums = column_part(current)
        totals = lax.psum((partial_sums[0], partial_sums[1]), "ba")
        current = column_apply(current, totals)
        if iteration + 1 < REPEAT_COUNT:
            partial_sums = sample_part(current)
            totals = lax.psum((partial_sums[0], partial_sums[1]), "ka")
            current = sample_apply(current, totals)
    raw_one, raw_two = raw_matrix(current)
    logit_one = first_view_logits / TEMP_PRED
    logit_two = second_view_logits / TEMP_PRED
    masses = lax.psum((jnp.sum(raw_one, axis=1), jnp.sum(raw_two, axis=1)), "ka")
    first_view_assignment = raw_one / masses[0][:, None]
    second_view_assignment = raw_two / masses[1][:, None]
    peaks = lax.pmax((jnp.max(logit_one, axis=1), jnp.max(logit_two, axis=1)), "ka")
    terms = lax.psum(
        (
            jnp.sum(jnp.exp(logit_one - peaks[0][:, None]), axis=1),
            jnp.sum(jnp.exp(logit_two - peaks[1][:, None]), axis=1),
            jnp.sum(first_view_assignment * logit_two, axis=1),
            jnp.sum(second_view_assignment * logit_one, axis=1),
        ),
        "ka",
    )
    lse_one = peaks[0] + jnp.log(terms[0])
    lse_two = peaks[1] + jnp.log(terms[1])
    row_loss = lse_two - terms[2] + lse_one - terms[3]
    return (K * first_view_assignment, row_loss)


def solution(mesh):
    placed = (P("ba", None), P("ba", None), P("ka", "ba"))
    return jax.shard_map(
        body, mesh=mesh, in_specs=placed, out_specs=(P("ba", "ka"), P("ba")), check_vma=False
    )
```

profile of v0, /device:TPU:0, one launch (start us, length us, event | category | flops | bytes accessed | tf_op | source)
XLA Modules:
  0.0 154.9 jit_solution(16839468313270747781)
XLA Ops:
  0.6 1.2 fusion.5
  1.9 1.2 fusion.7
  3.0 33.0 %all_gather.3 = f32[750,128]{0,1:T(8,128)S(1)} all-gather(f32[750,16]{0,1:T(8,128)} %param.5), channel_id=1, replica_groups=mesh['ba'=8,'ka'=4] {'ba'}, dimensions={1}, use_global_device_ids=true | all-gather | bytes 432000 | tf_op jit(solution)/shard_map/all_gather | solution.py:51
  36.1 1.7 %fusion.3 = (f32[750]{0:T(1024)S(1)}, f32[1024,750]{0,1:T(8,128)S(1)}) fusion(f32[750,128]{0,1:T(8,128)S(1)} %all_gather.3, f32[750]{0:T(1024)S(1)} %rsqrt.25, bf16[1024,128]{1,0:T(8,128)(2,1)} %param.3, f32[1024]{0:T(1024)S(1)} %rsqrt.24), kind=kOutput, calls=%fused_computation.22 | convolution fusion | flops 198728464 | bytes 3728240 | tf_op jit(solution)/shard_map/dot_general | solution.py:53
  37.8 2.6 %multiply_reduce_fusion.11 = (f32[1024]{0:T(1024)S(1)}, f32[750]{0:T(1024)S(1)}, f32[1024,750]{0,1:T(8,128)}) fusion(f32[750,128]{0,1:T(8,128)S(1)} %all_gather.3, f32[750]{0:T(1024)S(1)} %rsqrt.25, bf16[1024,128]{1,0:T(8,128)(2,1)S(1)} %copy-done.1, f32[1024]{0:T(1024)S(1)} %rsqrt.26), kind=kOutput, calls=%fused_computation.20 | convolution fusion | flops 200263440 | bytes 3732336 | tf_op jit(solution)/shard_map/dot_general | solution.py:54
  40.4 21.7 %all-reduce.2 = (f32[750]{0:T(1024)S(1)}, f32[750]{0:T(1024)S(1)}) all-reduce(f32[750]{0:T(1024)S(1)} %get-tuple-element.30, f32[750]{0:T(1024)S(1)} %get-tuple-element.7), channel_id=1, replica_groups=mesh['ba'=8,'ka'=4] {'ba'}, use_global_device_ids=true, to_apply=%region_3.0 | all-reduce | flops 1500 | bytes 12000 | tf_op jit(solution)/shard_map/psum | solution.py:63
  62.1 0.7 multiply_reduce_fusion.10
  62.8 5.8 %all-reduce.7 = (f32[1024]{0:T(1024)S(1)}, f32[1024]{0:T(1024)S(1)}) all-reduce(f32[1024]{0:T(1024)S(1)} %get-tuple-element.6, f32[1024]{0:T(1024)S(1)} %get-tuple-element.9), channel_id=1, replica_groups=mesh['ba'=8,'ka'=4] {'ka'}, use_global_device_ids=true, to_apply=%region_16.0 | all-reduce | flops 2048 | bytes 16384 | tf_op jit(solution)/shard_map/pmax | solution.py:75
  68.6 2.9 %exponential_reduce_fusion.1 = (f32[1024]{0:T(1024)S(1)}, f32[1024]{0:T(1024)S(1)}) fusion(f32[1024,750]{0,1:T(8,128)} %get-tuple-element.32, f32[1024]{0:T(1024)S(1)} %get-tuple-element.27, f32[750]{0:T(1024)S(1)} %broadcast_divide_fusion.6), kind=kLoop, calls=%fused_computation.9 | loop fusion | flops 4605952 | bytes 3087288 | tf_op jit(solution)/shard_map/reduce_sum | solution.py:79
  71.5 6.7 %all-reduce.6 = (f32[1024]{0:T(1024)S(1)}, f32[1024]{0:T(1024)S(1)}) all-reduce(f32[1024]{0:T(1024)S(1)} %get-tuple-element.10, f32[1024]{0:T(1024)S(1)} %get-tuple-element.5), channel_id=1, replica_groups=mesh['ba'=8,'ka'=4] {'ka'}, use_global_device_ids=true, to_apply=%region_5.0 | all-reduce | flops 2048 | bytes 16384 | tf_op jit(solution)/shard_map/psum | solution.py:67
  78.2 2.4 %multiply_reduce_fusion.3 = f32[750]{0:T(1024)S(1)} fusion(f32[1024]{0:T(1024)S(1)} %get-tuple-element.33, f32[1024,750]{0,1:T(8,128)} %get-tuple-element.32), kind=kLoop, calls=%fused_computation.4 | loop fusion | flops 2303250 | bytes 3079096 | tf_op jit(solution)/shard_map/reduce_sum | solution.py:22
  80.7 0.6 multiply_reduce_fusion.8
  81.3 17.4 %all-reduce.1 = (f32[750]{0:T(1024)S(1)}, f32[750]{0:T(1024)S(1)}) all-reduce(f32[750]{0:T(1024)S(1)} %multiply_reduce_fusion.8, f32[750]{0:T(1024)S(1)} %multiply_reduce_fusion.3), channel_id=1, replica_groups=mesh['ba'=8,'ka'=4] {'ba'}, use_global_device_ids=true, to_apply=%region_7.0 | all-reduce | flops 1500 | bytes 12000 | tf_op jit(solution)/shard_map/psum | solution.py:63
  99.2 1.3 copy-done
  101.1 5.8 %all-reduce.5 = (f32[1024]{0:T(1024)S(1)}, f32[1024]{0:T(1024)S(1)}) all-reduce(f32[1024]{0:T(1024)S(1)} %multiply_reduce_fusion.7, f32[1024]{0:T(1024)S(1)} %multiply_reduce_fusion.2), channel_id=1, replica_groups=mesh['ba'=8,'ka'=4] {'ka'}, use_global_device_ids=true, to_apply=%region_9.0 | all-reduce | flops 2048 | bytes 16384 | tf_op jit(solution)/shard_map/psum | solution.py:67
  106.9 2.4 %multiply_reduce_fusion.1 = f32[750]{0:T(1024)S(1)} fusion(f32[1024]{0:T(1024)S(1)} %broadcast_divide_fusion, f32[1024,750]{0,1:T(8,128)} %get-tuple-element.32), kind=kLoop, calls=%fused_computation.2 | loop fusion | flops 2303250 | bytes 3079096 | tf_op jit(solution)/shard_map/reduce_sum | solution.py:22
  109.3 0.6 multiply_reduce_fusion.6
  109.9 19.4 %all-reduce = (f32[750]{0:T(1024)S(1)}, f32[750]{0:T(1024)S(1)}) all-reduce(f32[750]{0:T(1024)S(1)} %multiply_reduce_fusion.6, f32[750]{0:T(1024)S(1)} %multiply_reduce_fusion.1), channel_id=1, replica_groups=mesh['ba'=8,'ka'=4] {'ba'}, use_global_device_ids=true, to_apply=%region_11.0 | all-reduce | flops 1500 | bytes 12000 | tf_op jit(solution)/shard_map/psum | solution.py:63
  129.3 2.5 %fusion.2 = f32[1024]{0:T(1024)S(1)} fusion(f32[750]{0:T(1024)S(1)} %broadcast_divide_fusion.4, f32[1024]{0:T(1024)S(1)} %broadcast_divide_fusion, f32[1024,750]{0,1:T(8,128)} %get-tuple-element.32), kind=kLoop, calls=%fused_computation.18 | loop fusion | flops 3070976 | bytes 3083192 | tf_op jit(solution)/shard_map/reduce_sum | solution.py:72
  131.8 0.6 fusion.1
  132.4 5.8 %all-reduce.4 = (f32[1024]{0:T(1024)S(1)}, f32[1024]{0:T(1024)S(1)}) all-reduce(f32[1024]{0:T(1024)S(1)} %fusion.1, f32[1024]{0:T(1024)S(1)} %fusion.2), channel_id=1, replica_groups=mesh['ba'=8,'ka'=4] {'ka'}, use_global_device_ids=true, to_apply=%region_13.0 | all-reduce | flops 2048 | bytes 16384 | tf_op jit(solution)/shard_map/psum | solution.py:72
  138.2 5.4 %multiply_reduce_fusion.5 = (f32[1024]{0:T(1024)S(1)}, f32[1024]{0:T(1024)S(1)}, f32[1024]{0:T(1024)S(1)}, f32[1024,750]{0,1:T(8,128)}) fusion(f32[1024,750]{0,1:T(8,128)} %get-tuple-element.32, f32[1024]{0:T(1024)S(1)} %get-tuple-element.21, f32[1024]{0:T(1024)S(1)} %broadcast_divide_fusion.2, f32[750]{0:T(1024)S(1)} %broadcast_divide_fusion.7, ...), kind=kLoop, calls=%fused_computation.8 | loop fusion | flops 13052928 | bytes 9254768 | tf_op jit(solution)/shard_map/reduce_sum | solution.py:80
  143.7 10.6 %all-reduce.3 = (f32[1024]{0:T(1024)S(1)}, f32[1024]{0:T(1024)S(1)}, f32[1024]{0:T(1024)S(1)}, f32[1024]{0:T(1024)S(1)}) all-reduce(f32[1024]{0:T(1024)S(1)} %get-tuple-element.3, f32[1024]{0:T(1024)S(1)} %get-tuple-element.8, f32[1024]{0:T(1024)S(1)} %get-tuple-element.2, ...), channel_id=1, replica_groups=mesh['ba'=8,'ka'=4] {'ka'}, use_global_device_ids=true, to_apply=%region_38.0 | all-reduce | flops 4096 | bytes 32768 | tf_op jit(solution)/shard_map/psum | solution.py:76
  154.3 0.6 add_subtract_fusion
  (18 shorter events, 1.2 us)
Async XLA Ops:
  0.6 37.2 %copy-start.1 = (bf16[1024,128]{1,0:T(8,128)(2,1)S(1)}, bf16[1024,128]{1,0:T(8,128)(2,1)}, u32[]{:S(2)}) copy-start(bf16[1024,128]{1,0:T(8,128)(2,1)} %param.4) | copy-start | bytes 786436
  98.6 1.9 %copy-start = (f32[1024,750]{0,1:T(8,128)S(1)}, f32[1024,750]{0,1:T(8,128)}, u32[]{:S(2)}) copy-start(f32[1024,750]{0,1:T(8,128)} %get-tuple-element.32) | copy-start | bytes 9216004
where the time goes:
time: 155 us
  blocking collectives  126 us (81%)
  other arithmetic  22.3 us (14%)
  matrix products  4.31 us (3%)
    psum x3, blocking collectives, body(): totals = lax.psum((partial_sums[0], partial_sums[1]), 'ba')  58.4 us
    all_gather x1, blocking collectives, body(): gathered = lax.all_gather(prototypes, 'ba', axis=1, tiled=True)  33 us
    psum x2, blocking collectives, body(): totals = lax.psum((partial_sums[0], partial_sums[1]), 'ka')  12.5 us
    psum x1, blocking collectives, body(): lax.psum((jnp.sum(jnp.exp(logit_one - peaks[0][:, None]), axis=1), jnp.su...  10.6 us
    pmax x1, blocking collectives, body(): lax.pmax((jnp.max(logit_one, axis=1), jnp.max(logit_two, axis=1)), 'ka')  5.77 us
    psum x1, blocking collectives, body(): lax.psum((jnp.sum(raw_one, axis=1), jnp.sum(raw_two, axis=1)), 'ka')  5.77 us
    reduce_sum x1, other arithmetic, body(): jnp.sum(first_view_assignment * logit_two, axis=1)  5.44 us
    reduce_sum x2, other arithmetic, vector_columns(): jnp.sum(kernel[1] * row_scale[1][:, None], axis=0)  4.9 us

commit v1 on v0

--- a/solution.py
+++ b/solution.py
@@ -48,7 +48,12 @@
 
 
 def body(emb_one, emb_two, prototypes):
-    gathered = lax.all_gather(prototypes, "ba", axis=1, tiled=True)
+    ring = [prototypes]
+    for hop in range(7):
+        ring.append(lax.ppermute(ring[-1], "ba", [(dev, (dev + 1) % 8) for dev in range(8)]))
+    gathered = jnp.roll(
+        jnp.concatenate(ring[::-1], axis=1), (lax.axis_index("ba") + 1) * ring[0].shape[1], axis=1
+    )
     centers = unit_rows(gathered)
     first_view_logits = jnp.dot(unit_rows(emb_one), centers.T, preferred_element_type=jnp.float32)
     second_view_logits = jnp.dot(unit_rows(emb_two), centers.T, preferred_element_type=jnp.float32)

time: 155 us -> 167 us (1.077)
  waiting for transfers between devices: 0 us -> 44 us
  blocking collectives: 126 us -> 89 us
  starting transfers between devices: 0 us -> 3.04 us
  local copies, waits for them, and re-layouts: 1.32 us -> 3.02 us
    ppermute x0 -> x7, waiting for transfers between devices: none -> 44 us  [body(): lax.ppermute(ring[-1], 'ba', [(dev, (dev + 1) % 8) for dev in range(8)])]
    all_gather x1 -> x0, blocking collectives: 33 us -> none  [body(): gathered = lax.all_gather(prototypes, 'ba', axis=1, tiled=True)]
    psum x3, blocking collectives: 58.4 us -> 54.1 us  [body(): totals = lax.psum((partial_sums[0], partial_sums[1]), 'ba')]
    ppermute x0 -> x7, starting transfers between devices: none -> 3.04 us  [body(): lax.ppermute(ring[-1], 'ba', [(dev, (dev + 1) % 8) for dev in range(8)])]
  transfers between devices with their start and end apart: 0 -> 7, of which waited for: 0 -> 7; matrix products, arithmetic and copies ran while one was open for 0% -> 1% of each run, Pallas kernels for 0% -> 0%
where the time goes in v1:
time: 167 us
  blocking collectives  89 us (53%)
  waiting for transfers between devices  44 us (26%)
  other arithmetic  22.3 us (13%)
  matrix products  4.31 us (3%)
  starting transfers between devices  3.04 us (2%)
  local copies, waits for them, and re-layouts  3.02 us (2%)
    psum x3, blocking collectives, body(): totals = lax.psum((partial_sums[0], partial_sums[1]), 'ba')  54.1 us
    ppermute x7, waiting for transfers between devices, body(): lax.ppermute(ring[-1], 'ba', [(dev, (dev + 1) % 8) for dev in range(8)])  44 us
    psum x2, blocking collectives, body(): totals = lax.psum((partial_sums[0], partial_sums[1]), 'ka')  12.9 us
    psum x1, blocking collectives, body(): lax.psum((jnp.sum(jnp.exp(logit_one - peaks[0][:, None]), axis=1), jnp.su...  10.5 us
    pmax x1, blocking collectives, body(): lax.pmax((jnp.max(logit_one, axis=1), jnp.max(logit_two, axis=1)), 'ka')  5.77 us
    psum x1, blocking collectives, body(): lax.psum((jnp.sum(raw_one, axis=1), jnp.sum(raw_two, axis=1)), 'ka')  5.77 us
    reduce_sum x1, other arithmetic, body(): jnp.sum(first_view_assignment * logit_two, axis=1)  5.44 us
    reduce_sum x2, other arithmetic, vector_columns(): jnp.sum(kernel[1] * row_scale[1][:, None], axis=0)  4.9 us
  transfers between devices with their start and end apart: 7, of which 7 were waited for; matrix products, arithmetic and copies ran while one was open for 1% of the time, Pallas kernels for 0%

profile of v1, /device:TPU:0, one launch (start us, length us, event | category | flops | bytes accessed | tf_op | source)
XLA Modules:
  0.0 166.6 jit_solution(8660189559560051593)
XLA Ops:
  0.6 3.0 %collective-permute-start = (f32[750,16]{0,1:T(8,128)}, f32[750,16]{0,1:T(8,128)S(1)}, u32[]{:S(2)}, u32[]{:S(2)}) collective-permute-start(f32[750,16]{0,1:T(8,128)} %param.5), channel_id=1, source_target_pairs={{0,4},{4,8},{8,12},{12,16},{16,20},{20,24},{24,28},{28,0},{1,5},{5... | collective-permute-start | bytes 144008 | tf_op jit(solution)/shard_map/ppermute | solution.py:53
  3.6 5.3 %collective-permute-done = f32[750,16]{0,1:T(8,128)S(1)} collective-permute-done((f32[750,16]{0,1:T(8,128)}, f32[750,16]{0,1:T(8,128)S(1)}, u32[]{:S(2)}, u32[]{:S(2)}) %collective-permute-start) | collective-permute-done | bytes 48032 | tf_op jit(solution)/shard_map/ppermute | solution.py:53
  9.0 6.8 %collective-permute-done.1 = f32[750,16]{0,1:T(8,128)S(1)} collective-permute-done((f32[750,16]{0,1:T(8,128)S(1)}, f32[750,16]{0,1:T(8,128)S(1)}, u32[]{:S(2)}, u32[]{:S(2)}) %collective-permute-start.1) | collective-permute-done | bytes 48032 | tf_op jit(solution)/shard_map/ppermute | solution.py:53
  15.8 6.8 %collective-permute-done.2 = f32[750,16]{0,1:T(8,128)S(1)} collective-permute-done((f32[750,16]{0,1:T(8,128)S(1)}, f32[750,16]{0,1:T(8,128)S(1)}, u32[]{:S(2)}, u32[]{:S(2)}) %collective-permute-start.2) | collective-permute-done | bytes 48032 | tf_op jit(solution)/shard_map/ppermute | solution.py:53
  22.5 6.8 %collective-permute-done.3 = f32[750,16]{0,1:T(8,128)S(1)} collective-permute-done((f32[750,16]{0,1:T(8,128)S(1)}, f32[750,16]{0,1:T(8,128)S(1)}, u32[]{:S(2)}, u32[]{:S(2)}) %collective-permute-start.3) | collective-permute-done | bytes 48032 | tf_op jit(solution)/shard_map/ppermute | solution.py:53
  29.3 7.1 %collective-permute-done.4 = f32[750,16]{0,1:T(8,128)S(1)} collective-permute-done((f32[750,16]{0,1:T(8,128)S(1)}, f32[750,16]{0,1:T(8,128)S(1)}, u32[]{:S(2)}, u32[]{:S(2)}) %collective-permute-start.4) | collective-permute-done | bytes 48032 | tf_op jit(solution)/shard_map/ppermute | solution.py:53
  37.6 5.6 %collective-permute-done.5 = f32[750,16]{0,1:T(8,128)S(1)} collective-permute-done((f32[750,16]{0,1:T(8,128)S(1)}, f32[750,16]{0,1:T(8,128)S(1)}, u32[]{:S(2)}, u32[]{:S(2)}) %collective-permute-start.5) | collective-permute-done | bytes 48032 | tf_op jit(solution)/shard_map/ppermute | solution.py:53
  44.5 5.6 %collective-permute-done.6 = f32[750,16]{0,1:T(8,128)S(1)} collective-permute-done((f32[750,16]{0,1:T(8,128)S(1)}, f32[750,16]{0,1:T(8,128)S(1)}, u32[]{:S(2)}, u32[]{:S(2)}) %collective-permute-start.6) | collective-permute-done | bytes 48032 | tf_op jit(solution)/shard_map/ppermute | solution.py:53
  51.9 1.7 %fusion.3 = (f32[750]{0:T(1024)S(1)}, f32[1024,750]{0,1:T(8,128)S(1)}) fusion(f32[750,256]{0,1:T(8,128)S(1)} %constant_dynamic-update-slice_fusion, s32[]{:T(128)S(6)} %select_n.14, f32[750]{0:T(1024)S(1)} %rsqrt.25, bf16[1024,128]{1,0:T(8,128)(2,1)} %param.3, f32[1024]{0:T(1024)S(1)} %rsqrt.24), kind=kOutput, calls=%fused_computation.22 | convolution fusion | flops 198728464 | bytes 3738556 | tf_op jit(solution)/shard_map/dot_general | solution.py:58
  53.6 2.6 %multiply_reduce_fusion.11 = (f32[1024]{0:T(1024)S(1)}, f32[750]{0:T(1024)S(1)}, f32[1024,750]{0,1:T(8,128)}) fusion(f32[750,256]{0,1:T(8,128)S(1)} %constant_dynamic-update-slice_fusion, s32[]{:T(128)S(6)} %select_n.14, f32[750]{0:T(1024)S(1)} %rsqrt.25, bf16[1024,128]{1,0:T(8,128)(2,1)S(1)} %copy-done.1, f32[1024]{0:T(1024)S(1)} %rsqrt.26), kind=kOutput, calls=%fused_computation.20 | convolution fusion | flops 200263440 | bytes 3742652 | tf_op jit(solution)/shard_map/dot_general | solution.py:59
  56.2 17.4 %all-reduce.2 = (f32[750]{0:T(1024)S(1)}, f32[750]{0:T(1024)S(1)}) all-reduce(f32[750]{0:T(1024)S(1)} %get-tuple-element.30, f32[750]{0:T(1024)S(1)} %get-tuple-element.7), channel_id=1, replica_groups=mesh['ba'=8,'ka'=4] {'ba'}, use_global_device_ids=true, to_apply=%region_3.4 | all-reduce | flops 1500 | bytes 12000 | tf_op jit(solution)/shard_map/psum | solution.py:68
  74.3 5.8 %all-reduce.7 = (f32[1024]{0:T(1024)S(1)}, f32[1024]{0:T(1024)S(1)}) all-reduce(f32[1024]{0:T(1024)S(1)} %get-tuple-element.6, f32[1024]{0:T(1024)S(1)} %get-tuple-element.9), channel_id=1, replica_groups=mesh['ba'=8,'ka'=4] {'ka'}, use_global_device_ids=true, to_apply=%region_16.17 | all-reduce | flops 2048 | bytes 16384 | tf_op jit(solution)/shard_map/pmax | solution.py:80
  80.1 2.9 %exponential_reduce_fusion.1 = (f32[1024]{0:T(1024)S(1)}, f32[1024]{0:T(1024)S(1)}) fusion(f32[1024,750]{0,1:T(8,128)} %get-tuple-element.32, f32[1024]{0:T(1024)S(1)} %get-tuple-element.27, f32[750]{0:T(1024)S(1)} %broadcast_divide_fusion.6), kind=kLoop, calls=%fused_computation.9 | loop fusion | flops 4605952 | bytes 3087288 | tf_op jit(solution)/shard_map/reduce_sum | solution.py:84
  83.0 7.1 %all-reduce.6 = (f32[1024]{0:T(1024)S(1)}, f32[1024]{0:T(1024)S(1)}) all-reduce(f32[1024]{0:T(1024)S(1)} %get-tuple-element.10, f32[1024]{0:T(1024)S(1)} %get-tuple-element.5), channel_id=1, replica_groups=mesh['ba'=8,'ka'=4] {'ka'}, use_global_device_ids=true, to_apply=%region_5.6 | all-reduce | flops 2048 | bytes 16384 | tf_op jit(solution)/shard_map/psum | solution.py:72
  90.1 2.4 %multiply_reduce_fusion.3 = f32[750]{0:T(1024)S(1)} fusion(f32[1024]{0:T(1024)S(1)} %get-tuple-element.33, f32[1024,750]{0,1:T(8,128)} %get-tuple-element.32), kind=kLoop, calls=%fused_computation.4 | loop fusion | flops 2303250 | bytes 3079096 | tf_op jit(solution)/shard_map/reduce_sum | solution.py:22
  93.1 19.4 %all-reduce.1 = (f32[750]{0:T(1024)S(1)}, f32[750]{0:T(1024)S(1)}) all-reduce(f32[750]{0:T(1024)S(1)} %multiply_reduce_fusion.8, f32[750]{0:T(1024)S(1)} %multiply_reduce_fusion.3), channel_id=1, replica_groups=mesh['ba'=8,'ka'=4] {'ba'}, use_global_device_ids=true, to_apply=%region_7.8 | all-reduce | flops 1500 | bytes 12000 | tf_op jit(solution)/shard_map/psum | solution.py:68
  113.1 1.3 copy-done
  114.9 5.8 %all-reduce.5 = (f32[1024]{0:T(1024)S(1)}, f32[1024]{0:T(1024)S(1)}) all-reduce(f32[1024]{0:T(1024)S(1)} %multiply_reduce_fusion.7, f32[1024]{0:T(1024)S(1)} %multiply_reduce_fusion.2), channel_id=1, replica_groups=mesh['ba'=8,'ka'=4] {'ka'}, use_global_device_ids=true, to_apply=%region_9.10 | all-reduce | flops 2048 | bytes 16384 | tf_op jit(solution)/shard_map/psum | solution.py:72
  120.7 2.4 %multiply_reduce_fusion.1 = f32[750]{0:T(1024)S(1)} fusion(f32[1024]{0:T(1024)S(1)} %broadcast_divide_fusion, f32[1024,750]{0,1:T(8,128)} %get-tuple-element.32), kind=kLoop, calls=%fused_computation.2 | loop fusion | flops 2303250 | bytes 3079096 | tf_op jit(solution)/shard_map/reduce_sum | solution.py:22
  123.7 17.4 %all-reduce = (f32[750]{0:T(1024)S(1)}, f32[750]{0:T(1024)S(1)}) all-reduce(f32[750]{0:T(1024)S(1)} %multiply_reduce_fusion.6, f32[750]{0:T(1024)S(1)} %multiply_reduce_fusion.1), channel_id=1, replica_groups=mesh['ba'=8,'ka'=4] {'ba'}, use_global_device_ids=true, to_apply=%region_11.12 | all-reduce | flops 1500 | bytes 12000 | tf_op jit(solution)/shard_map/psum | solution.py:68
  141.2 2.5 %fusion.2 = f32[1024]{0:T(1024)S(1)} fusion(f32[750]{0:T(1024)S(1)} %broadcast_divide_fusion.4, f32[1024]{0:T(1024)S(1)} %broadcast_divide_fusion, f32[1024,750]{0,1:T(8,128)} %get-tuple-element.32), kind=kLoop, calls=%fused_computation.18 | loop fusion | flops 3070976 | bytes 3083192 | tf_op jit(solution)/shard_map/reduce_sum | solution.py:77
  144.3 5.8 %all-reduce.4 = (f32[1024]{0:T(1024)S(1)}, f32[1024]{0:T(1024)S(1)}) all-reduce(f32[1024]{0:T(1024)S(1)} %fusion.1, f32[1024]{0:T(1024)S(1)} %fusion.2), channel_id=1, replica_groups=mesh['ba'=8,'ka'=4] {'ka'}, use_global_device_ids=true, to_apply=%region_13.14 | all-reduce | flops 2048 | bytes 16384 | tf_op jit(solution)/shard_map/psum | solution.py:77
  150.1 5.4 %multiply_reduce_fusion.5 = (f32[1024]{0:T(1024)S(1)}, f32[1024]{0:T(1024)S(1)}, f32[1024]{0:T(1024)S(1)}, f32[1024,750]{0,1:T(8,128)}) fusion(f32[1024,750]{0,1:T(8,128)} %get-tuple-element.32, f32[1024]{0:T(1024)S(1)} %get-tuple-element.21, f32[1024]{0:T(1024)S(1)} %broadcast_divide_fusion.2, f32[750]{0:T(1024)S(1)} %broadcast_divide_fusion.7, ...), kind=kLoop, calls=%fused_computation.8 | loop fusion | flops 13052928 | bytes 9254768 | tf_op jit(solution)/shard_map/reduce_sum | solution.py:85
  155.5 10.5 %all-reduce.3 = (f32[1024]{0:T(1024)S(1)}, f32[1024]{0:T(1024)S(1)}, f32[1024]{0:T(1024)S(1)}, f32[1024]{0:T(1024)S(1)}) all-reduce(f32[1024]{0:T(1024)S(1)} %get-tuple-element.3, f32[1024]{0:T(1024)S(1)} %get-tuple-element.8, f32[1024]{0:T(1024)S(1)} %get-tuple-element.2, ...), channel_id=1, replica_groups=mesh['ba'=8,'ka'=4] {'ka'}, use_global_device_ids=true, to_apply=%region_38.39 | all-reduce | flops 4096 | bytes 32768 | tf_op jit(solution)/shard_map/psum | solution.py:81
  (47 shorter events, 8.3 us)
Async XLA Ops:
  0.6 8.3 %collective-permute-start = (f32[750,16]{0,1:T(8,128)}, f32[750,16]{0,1:T(8,128)S(1)}, u32[]{:S(2)}, u32[]{:S(2)}) collective-permute-start(f32[750,16]{0,1:T(8,128)} %param.5), channel_id=1, source_target_pairs={{0,4},{4,8},{8,12},{12,16},{16,20},{20,24},{24,28},{28,0},{1,5},{5... | collective-permute-start | bytes 144008 | tf_op jit(solution)/shard_map/ppermute | solution.py:53
  9.0 6.8 %collective-permute-start.1 = (f32[750,16]{0,1:T(8,128)S(1)}, f32[750,16]{0,1:T(8,128)S(1)}, u32[]{:S(2)}, u32[]{:S(2)}) collective-permute-start(f32[750,16]{0,1:T(8,128)S(1)} %collective-permute-done), channel_id=1, source_target_pairs={{0,4},{4,8},{8,12},{12,16},{16,20},{20,24},{24,28},{28,0},{1,5},{5... | collective-permute-start | bytes 144008 | tf_op jit(solution)/shard_map/ppermute | solution.py:53
  15.8 6.8 %collective-permute-start.2 = (f32[750,16]{0,1:T(8,128)S(1)}, f32[750,16]{0,1:T(8,128)S(1)}, u32[]{:S(2)}, u32[]{:S(2)}) collective-permute-start(f32[750,16]{0,1:T(8,128)S(1)} %collective-permute-done.1), channel_id=1, source_target_pairs={{0,4},{4,8},{8,12},{12,16},{16,20},{20,24},{24,28},{28,0},{1,5},{5... | collective-permute-start | bytes 144008 | tf_op jit(solution)/shard_map/ppermute | solution.py:53
  22.5 6.8 %collective-permute-start.3 = (f32[750,16]{0,1:T(8,128)S(1)}, f32[750,16]{0,1:T(8,128)S(1)}, u32[]{:S(2)}, u32[]{:S(2)}) collective-permute-start(f32[750,16]{0,1:T(8,128)S(1)} %collective-permute-done.2), channel_id=1, source_target_pairs={{0,4},{4,8},{8,12},{12,16},{16,20},{20,24},{24,28},{28,0},{1,5},{5... | collective-permute-start | bytes 144008 | tf_op jit(solution)/shard_map/ppermute | solution.py:53
  29.3 7.1 %collective-permute-start.4 = (f32[750,16]{0,1:T(8,128)S(1)}, f32[750,16]{0,1:T(8,128)S(1)}, u32[]{:S(2)}, u32[]{:S(2)}) collective-permute-start(f32[750,16]{0,1:T(8,128)S(1)} %collective-permute-done.3), channel_id=1, source_target_pairs={{0,4},{4,8},{8,12},{12,16},{16,20},{20,24},{24,28},{28,0},{1,5},{5... | collective-permute-start | bytes 144008 | tf_op jit(solution)/shard_map/ppermute | solution.py:53
  36.5 6.8 %collective-permute-start.5 = (f32[750,16]{0,1:T(8,128)S(1)}, f32[750,16]{0,1:T(8,128)S(1)}, u32[]{:S(2)}, u32[]{:S(2)}) collective-permute-start(f32[750,16]{0,1:T(8,128)S(1)} %collective-permute-done.4), channel_id=1, source_target_pairs={{0,4},{4,8},{8,12},{12,16},{16,20},{20,24},{24,28},{28,0},{1,5},{5... | collective-permute-start | bytes 144008 | tf_op jit(solution)/shard_map/ppermute | solution.py:53
  37.6 16.0 %copy-start.1 = (bf16[1024,128]{1,0:T(8,128)(2,1)S(1)}, bf16[1024,128]{1,0:T(8,128)(2,1)}, u32[]{:S(2)}) copy-start(bf16[1024,128]{1,0:T(8,128)(2,1)} %param.4) | copy-start | bytes 786436
  43.2 6.8 %collective-permute-start.6 = (f32[750,16]{0,1:T(8,128)S(1)}, f32[750,16]{0,1:T(8,128)S(1)}, u32[]{:S(2)}, u32[]{:S(2)}) collective-permute-start(f32[750,16]{0,1:T(8,128)S(1)} %collective-permute-done.5), channel_id=1, source_target_pairs={{0,4},{4,8},{8,12},{12,16},{16,20},{20,24},{24,28},{28,0},{1,5},{5... | collective-permute-start | bytes 144008 | tf_op jit(solution)/shard_map/ppermute | solution.py:53
  112.5 1.9 %copy-start = (f32[1024,750]{0,1:T(8,128)S(1)}, f32[1024,750]{0,1:T(8,128)}, u32[]{:S(2)}) copy-start(f32[1024,750]{0,1:T(8,128)} %get-tuple-element.32) | copy-start | bytes 9216004
